TPU v7x, 32 devices: a whole 2x2x4 slice. The times are simulated.
32 devices in a mesh: cuts: 8 (over z, y), event: 4 (over x, core).
Axes of the slice: x: 2, y: 2, z: 4, core: 2. Of those that a mesh axis runs over, the one named last changes fastest.
Arguments:
- kernels: float32 [4, 64, 128, 256], P('event', 'cuts'), may hold values from -24 to 24
- steps: float32 [8, 64, 128, 256], P(None, 'cuts', 'event'), may hold values from -11 to 11
- curvature: float32 [8, 64, 128, 256], P(None, 'cuts', 'event'), may hold values from 0.2 to 5
Outputs:
- gradient: float32 [64, 128, 256], P('cuts', 'event')
- direction: float32 [64, 128, 256], P('cuts', 'event')
All inputs are finite; a program needn't handle non-finite values.
Results may differ from a plain program's by a relative error of at most 0.00021.
Values sent between devices are 32-bit elements; how exact they have to be, the bound alone decides.
A program may use at most 64 MiB of HBM per device.

v0:
```python
import math

import jax
import jax.numpy as jnp
from jax import lax
from jax.sharding import PartitionSpec as P

PAIRS = 8
RIM = 4


def with_halo(cells, sides, width):
    for axis, dim in sides:
        count = lax.axis_size(axis)
        head = lax.slice_in_dim(cells, 0, width, axis=dim)
        tail = lax.slice_in_dim(cells, cells.shape[dim] - width, cells.shape[dim], axis=dim)
        cells = jnp.concatenate(
            [
                lax.ppermute(tail, axis, [(i, (i + 1) % count) for i in range(count)]),
                cells,
                lax.ppermute(head, axis, [((i + 1) % count, i) for i in range(count)]),
            ],
            axis=dim,
        )
    return cells


def gauss_matrix(length, sigma):
    points = jnp.arange(length, dtype=jnp.float32)
    offset = points[:, None] - points[None, :]
    matrix = jnp.exp(-offset * offset / (2.0 * sigma * sigma))
    return matrix / jnp.sum(matrix, axis=1, keepdims=True)


def cycle_weights():
    unscaled = [math.exp(-((column - RIM) ** 2) / 4.5) for column in range(2 * RIM + 1)]
    whole = sum(unscaled)
    return [weight / whole for weight in unscaled]


def smooth_plane(field):
    lat_len = field.shape[2]
    plane = jnp.dot(
        field.reshape(-1, lat_len), gauss_matrix(lat_len, 4.0).T, precision=lax.Precision.HIGHEST
    ).reshape(field.shape)
    padded = with_halo(plane, (("cuts", 0),), RIM)
    lon_len = plane.shape[0]
    weights = cycle_weights()
    smoothed = jnp.zeros_like(plane)
    for column in range(2 * RIM + 1):
        smoothed = smoothed + weights[column] * padded[column : column + lon_len]
    return smoothed


def shards(kernels, steps, curvature):
    partial_value = kernels[0]
    rad_len = partial_value.shape[1]
    radial = jnp.einsum(
        "ij,ajb->aib", gauss_matrix(rad_len, 3.0), partial_value, precision=lax.Precision.HIGHEST
    )
    summed = lax.psum(radial, "event")
    smoothed = smooth_plane(summed)
    portion = rad_len // lax.axis_size("event")
    gradient = lax.dynamic_slice_in_dim(smoothed, lax.axis_index("event") * portion, portion, 1)
    changes = curvature * steps
    vectors = jnp.concatenate(
        [steps.reshape(PAIRS, -1), changes.reshape(PAIRS, -1), gradient.reshape(1, -1)], axis=0
    )
    products = lax.psum(
        jnp.dot(vectors, vectors.T, precision=lax.Precision.HIGHEST), ("cuts", "event")
    )
    curvs = jnp.diagonal(products[:PAIRS, PAIRS : 2 * PAIRS])
    inverse = 1.0 / curvs
    scaling = curvs[PAIRS - 1] / products[2 * PAIRS - 1, 2 * PAIRS - 1]
    weights_now = jnp.zeros((2 * PAIRS + 1,), jnp.float32).at[2 * PAIRS].set(1.0)
    alphas = [None] * PAIRS
    for pair in reversed(range(PAIRS)):
        alphas[pair] = inverse[pair] * jnp.dot(
            products[pair], weights_now, precision=lax.Precision.HIGHEST
        )
        weights_now = weights_now.at[PAIRS + pair].add(-alphas[pair])
    weights_now = scaling * weights_now
    for pair in range(PAIRS):
        second = inverse[pair] * jnp.dot(
            products[PAIRS + pair], weights_now, precision=lax.Precision.HIGHEST
        )
        weights_now = weights_now.at[pair].add(alphas[pair] - second)
    direction = -jnp.dot(weights_now[None, :], vectors, precision=lax.Precision.HIGHEST).reshape(
        gradient.shape
    )
    return (gradient, direction)


def solution(mesh):
    placed = (
        P("event", "cuts", None, None),
        P(None, "cuts", "event", None),
        P(None, "cuts", "event", None),
    )
    return jax.shard_map(
        shards,
        mesh=mesh,
        in_specs=placed,
        out_specs=(P("cuts", "event", None), P("cuts", "event", None)),
        check_vma=False,
    )
```

profile of v0, /device:TPU:0, one launch (start us, length us, event | category | flops | bytes accessed | tf_op | source)
XLA Modules:
  0.0 200.9 jit_solution(306684947524946787)
XLA Ops:
  7.2 0.0 copy-start
  7.2 0.0 all-reduce.2.cloned.1.call-start
  7.2 0.1 fusion.36
  7.4 1.0 copy-done
  8.4 2.0 %fusion.11 = f32[128,8,256]{2,0,1:T(8,128)} fusion(f32[1,8,128,256]{3,2,1,0:T(8,128)S(1)} %copy-done, f32[128]{0:T(128)S(1)} %fusion.36), kind=kOutput, calls=%fused_computation.27 | convolution fusion | flops 402735104 | bytes 2097664 | tf_op jit(solution)/shard_map/ij,ajb->aib/dot_general | solution.py:58
  10.4 0.0 all-reduce.2.cloned.1.call-update
  10.5 1.2 copy.40
  11.7 1.5 constant_dynamic-update-slice_fusion.1
  13.2 0.4 mul.113
  13.6 2.6 %copy.41 = f32[1,8,256,256]{3,1,2,0:T(8,128)} copy(f32[1,8,256,256]{3,2,1,0:T(8,128)S(1)} %bitcast.165) | data formatting | bytes 4194304
  16.2 0.2 fusion.28
  16.4 33.3 %all-reduce.2.cloned.1.call-done = f32[1024,256]{1,0:T(8,128)} async-done(((f32[1024,256]{1,0:T(8,128)}), f32[1024,256]{1,0:T(8,128)}) %all-reduce.2.cloned.1.call-update) | async-done | bytes 1048592 | tf_op jit(solution)/shard_map/psum | solution.py:61
  49.6 2.5 %fusion.25 = f32[1024,256]{1,0:T(8,128)S(1)} fusion(f32[1024,256]{1,0:T(8,128)} %all-reduce.2.cloned.1.call-done, f32[256]{0:T(256)S(1)} %fusion.28), kind=kOutput, calls=%fused_computation.48 | convolution fusion | flops 805634048 | bytes 2098176 | tf_op jit(solution)/shard_map/dot_general | solution.py:43
  52.1 0.9 fusion.74
  53.0 1.5 collective-permute-start
  54.5 3.2 %collective-permute-start.1 = (f32[4,128,256]{2,1,0:T(8,128)}, f32[4,128,256]{2,1,0:T(8,128)S(1)}, u32[]{:S(2)}, u32[]{:S(2)}) collective-permute-start(f32[4,128,256]{2,1,0:T(8,128)} %bitcast.6), channel_id=1, source_target_pairs={{4,0},{8,4},{12,8},{16,12},{20,16},{24,20},{28,24},{0,28},{5,1},{9... | collective-permute-start | bytes 1572872 | tf_op jit(solution)/shard_map/ppermute | solution.py:21
  57.7 1.4 constant_dynamic-update-slice_fusion
  59.2 19.6 %collective-permute-done.1 = f32[4,128,256]{2,1,0:T(8,128)S(1)} collective-permute-done((f32[4,128,256]{2,1,0:T(8,128)}, f32[4,128,256]{2,1,0:T(8,128)S(1)}, u32[]{:S(2)}, u32[]{:S(2)}) %collective-permute-start.1) | collective-permute-done | bytes 524320 | tf_op jit(solution)/shard_map/ppermute | solution.py:21
  78.7 0.3 pad_slice_fusion.4
  79.1 2.1 %fusion.4 = (f32[8,128,256]{2,1,0:T(8,128)S(1)}, f32[8,128,256]{2,1,0:T(8,128)S(1)}, f32[8,128,256]{2,1,0:T(8,128)S(1)}, f32[8,128,256]{2,1,0:T(8,128)S(1)}, f32[8,128,256]{2,1,0:T(8,128)S(1)}) fusion(f32[8,128,256]{2,1,0:T(8,128)S(1)} %bitcast.161, f32[4,128,256]{2,1,0:T(8,128)} %collective-permute-done), kind=kLoop, calls=%fused_computation.17 | loop fusion | flops 2621440 | bytes 6815744 | tf_op jit(solution)/shard_map/add | solution.py:51
  81.2 0.2 fusion.17
  81.4 0.3 reshape.412
  81.7 6.0 %dynamic-update-slice.38 = f32[17,65536]{1,0:T(8,128)} dynamic-update-slice(f32[17,65536]{1,0:T(8,128)} %constant_dynamic-update-slice_fusion, f32[1,65536]{1,0:T(1,128)S(1)} %reshape.412, s32[]{} %constant.465, s32[]{} %constant.463) | dynamic-update-slice | bytes 524292 | tf_op jit(solution)/shard_map/concatenate | solution.py:66
  87.7 8.8 %fusion.76 = f32[17,17]{1,0:T(8,128)S(1)} fusion(f32[17,65536]{1,0:T(8,128)} %dynamic-update-slice.38), kind=kOutput, calls=%fused_computation.135 | convolution fusion | flops 227278848 | bytes 4457604 | tf_op jit(solution)/shard_map/dot_general | solution.py:70
  96.5 39.4 %psum.15 = f32[17,17]{1,0:T(8,128)S(1)} all-reduce(f32[17,17]{1,0:T(8,128)S(1)} %fusion.76), channel_id=1, replica_groups=mesh['cuts'=8,'event'=4] {'cuts','event'}, use_global_device_ids=true, to_apply=%region_3.0 | all-reduce | flops 289 | bytes 2312 | tf_op jit(solution)/shard_map/psum | solution.py:69
  135.9 0.1 slice.401
  136.0 0.6 gather_fusion
  136.6 0.6 slice.344
  137.2 0.6 slice.402
  137.8 0.7 fusion.75
  138.5 0.6 fusion.70
  140.3 1.3 fusion.68
  142.9 0.2 constant_dynamic-update-slice_fusion.14
  143.1 1.3 fusion.66
  145.7 0.2 constant_dynamic-update-slice_fusion.13
  145.8 1.3 fusion.64
  148.4 0.2 constant_dynamic-update-slice_fusion.12
  148.6 1.3 fusion.62
  151.1 0.2 constant_dynamic-update-slice_fusion.11
  151.3 1.3 fusion.60
  153.9 0.2 constant_dynamic-update-slice_fusion.10
  154.1 1.3 fusion.58
  156.6 0.2 constant_dynamic-update-slice_fusion.9
  156.8 1.3 fusion.56
  159.4 0.2 constant_dynamic-update-slice_fusion.8
  160.7 1.3 fusion.54
  163.2 1.3 fusion.52
  165.8 0.2 constant_dynamic-update-slice_fusion.7
  166.0 1.4 fusion.50
  168.6 0.2 constant_dynamic-update-slice_fusion.6
  168.8 1.4 fusion.48
  171.4 0.2 add_dynamic-update-slice_fusion.1
  171.6 1.3 fusion.46
  174.1 0.2 constant_dynamic-update-slice_fusion.5
  174.2 1.3 fusion.44
  176.8 0.2 constant_dynamic-update-slice_fusion.4
  177.0 1.4 fusion.42
  179.6 0.2 constant_dynamic-update-slice_fusion.3
  179.7 1.3 fusion.40
  182.3 0.2 add_dynamic-update-slice_fusion
  182.4 4.8 %copy.42 = f32[3,8,256,256]{3,2,1,0:T(8,128)S(1)} copy(f32[3,8,256,256]{3,1,2,0:T(8,128)} %bitcast.159) | data formatting | bytes 12582912
  187.2 0.4 slice.419
  187.7 5.6 %fusion = f32[1,8,32,256]{3,0,2,1:T(1,128)S(1)} fusion(f32[8,32,256,17]{2,1,0,3:T(8,128)S(1)} %bitcast.160, f32[17]{0:T(128)S(1)} %add_dynamic-update-slice_fusion), kind=kOutput, calls=%fused_computation.1 | convolution fusion | flops 13369344 | bytes 4718660 | tf_op jit(solution)/shard_map/dot_general | solution.py:88
  193.3 0.7 bitcast_negate_fusion
  (18 shorter events, 0.1 us)
Async XLA Ops:
  7.2 1.2 copy-start
  7.2 3.3 %copy-start.1 = (f32[8,8,32,256]{3,2,1,0:T(8,128)S(1)}, f32[8,8,32,256]{3,2,1,0:T(8,128)}, u32[]{:S(2)}) copy-start(f32[8,8,32,256]{3,2,1,0:T(8,128)} %param.38) | copy-start | bytes 6291460
  7.2 42.4 %all-reduce.2.cloned.1.call-start = ((), (), s32[]{:S(2)}) async-start(), calls=%async_computation | async-start | bytes 2097152 | tf_op jit(solution)/shard_map/psum | solution.py:61
  10.5 2.7 %copy-start.3 = (f32[8,8,32,256]{3,2,1,0:T(8,128)S(1)}, f32[8,8,32,256]{3,2,1,0:T(8,128)}, u32[]{:S(2)}) copy-start(f32[8,8,32,256]{3,2,1,0:T(8,128)} %param.39) | copy-start | bytes 6291460
  16.2 43.0 %copy-start.6 = (f32[17]{0:T(128)S(1)}, f32[17]{0:T(128)}, u32[]{:S(2)}) copy-start(f32[17]{0:T(128)} %constant.416.clone.1) | copy-start | bytes 208
  49.6 8.1 %copy-start.2 = (f32[1,8,256,256]{3,1,2,0:T(8,128)S(1)}, f32[1,8,256,256]{3,1,2,0:T(8,128)}, u32[]{:S(2)}) copy-start(f32[1,8,256,256]{3,1,2,0:T(8,128)} %copy.41) | copy-start | bytes 6291460
  53.0 26.0 %collective-permute-start = (f32[4,128,256]{2,1,0:T(8,128)S(1)}, f32[4,128,256]{2,1,0:T(8,128)}, u32[]{:S(2)}, u32[]{:S(2)}) collective-permute-start(f32[4,128,256]{2,1,0:T(8,128)S(1)} %bitcast.169), channel_id=1, source_target_pairs={{0,4},{4,8},{8,12},{12,16},{16,20},{20,24},{24,28},{28,0},{1,5},{5... | collective-permute-start | bytes 1572872 | tf_op jit(solution)/shard_map/ppermute | solution.py:19
  54.5 24.2 %collective-permute-start.1 = (f32[4,128,256]{2,1,0:T(8,128)}, f32[4,128,256]{2,1,0:T(8,128)S(1)}, u32[]{:S(2)}, u32[]{:S(2)}) collective-permute-start(f32[4,128,256]{2,1,0:T(8,128)} %bitcast.6), channel_id=1, source_target_pairs={{4,0},{8,4},{12,8},{16,12},{20,16},{24,20},{28,24},{0,28},{5,1},{9... | collective-permute-start | bytes 1572872 | tf_op jit(solution)/shard_map/ppermute | solution.py:21
  81.4 15.1 %copy-start.4 = (f32[8,32,256]{2,1,0:T(8,128)}, f32[8,32,256]{2,1,0:T(8,128)S(1)}, u32[]{:S(2)}) copy-start(f32[8,32,256]{2,1,0:T(8,128)S(1)} %fusion.17) | copy-start | bytes 786436
  135.9 4.4 %copy-start.5 = (f32[17,17]{1,0:T(8,128)}, f32[17,17]{1,0:T(8,128)S(1)}, u32[]{:S(2)}) copy-start(f32[17,17]{1,0:T(8,128)S(1)} %psum.15) | copy-start | bytes 3472
Sparse Core Ops, SparseCore 0:
  10.6 39.0 all-reduce.1
where the time goes:
time: 202 us; the launch traced here: 201 us
  waiting for transfers between devices  52.8 us (26%)
  blocking collectives  39.4 us (20%)
  between operations  35.5 us (18%)
  other arithmetic  26.4 us (13%)
  local copies, waits for them, and re-layouts  23.1 us (11%)
  matrix products  18.9 us (9%)
  starting transfers between devices  4.76 us (2%)
    psum x1, blocking collectives, shards(): lax.psum(jnp.dot(vectors, vectors.T, precision=lax.Precision.HIGHEST), ('...  39.4 us
    psum x1, waiting for transfers between devices, shards(): summed = lax.psum(radial, 'event')  33.3 us
    ppermute x1, waiting for transfers between devices, with_halo(): lax.ppermute(head, axis, [((i + 1) % count, i) for i in range(count)])  19.6 us
    unnamed x21, local copies, waits for them, and re-layouts  13 us
    dot_general x8, other arithmetic, shards(): jnp.dot(products[PAIRS + pair], weights_now, precision=lax.Precision.HIGH...  10.6 us
    dot_general x8, other arithmetic, shards(): jnp.dot(products[pair], weights_now, precision=lax.Precision.HIGHEST)  9.85 us
    dot_general x1, matrix products, shards(): jnp.dot(vectors, vectors.T, precision=lax.Precision.HIGHEST)  8.77 us
    concatenate x1, local copies, waits for them, and re-layouts, shards(): jnp.concatenate([steps.reshape(PAIRS, -1), changes.reshape(PAIRS, -1), gr...  6.03 us
  transfers between devices with their start and end apart: 3, of which 2 were waited for; matrix products, arithmetic and copies ran while one was open for 4% of the time, Pallas kernels for 0%

commit v1 on v0

v1 whole, which is shorter than its diff:
```python
import functools
import math

import jax
import jax.numpy as jnp
from jax import lax
from jax.experimental import pallas as pl
from jax.experimental.pallas import tpu as pltpu
from jax.sharding import PartitionSpec as P

RIM = 4
LANES = 128
SUB = 8
MESH = pl.DeviceIdType.MESH
HIGHEST = lax.Precision.HIGHEST


def cycle_weights():
    unscaled = [math.exp(-((column - RIM) ** 2) / 4.5) for column in range(2 * RIM + 1)]
    whole = sum(unscaled)
    return [weight / whole for weight in unscaled]


def halves(value):
    high = value.astype(jnp.bfloat16)
    return high, (value - high.astype(jnp.float32)).astype(jnp.bfloat16)


def unscaled_gauss(length, sigma):
    rows = lax.broadcasted_iota(jnp.int32, (length, length), 0)
    columns = lax.broadcasted_iota(jnp.int32, (length, length), 1)
    offset = (rows - columns).astype(jnp.float32)
    return jnp.exp(-offset * offset / (2.0 * sigma * sigma))


def upper(pairs):
    return [(i, j) for i in range(pairs) for j in range(i, pairs)]


def kernel(
    sizes,
    kern_hbm, steps_hbm, curv_hbm, grad_hbm, dir_hbm,
    kern, steps, changes, rad, far_in, near_in, far_out, x_in, plane, lead_in, trail_in,
    grad, direc, rad_mat, lat_mat, gram_acc, gram_tile, gram_event, gram_part, gram_cuts,
    table, splat, mix, coef, late_tile, late_event, late_part, late_cuts,
    load_sem, out_sem, core_send, core_recv, x_send, x_recv, halo_send, halo_recv,
    ge_send, ge_recv, gc_send, gc_recv, le_send, le_recv, lc_send, lc_recv,
):
    n_c, n_e, pairs, rad_len, lat_len = sizes
    part = rad_len // n_e
    c = lax.axis_index("cuts")
    e = lax.axis_index("event")
    barrier = pltpu.get_barrier_semaphore()
    for d in range(1, n_e):
        pl.semaphore_signal(barrier, 1, device_id={"event": lax.rem(e + d, n_e)}, device_id_type=MESH)
    for d in range(1, n_c):
        pl.semaphore_signal(barrier, 1, device_id={"cuts": lax.rem(c + d, n_c)}, device_id_type=MESH)

    loads = [
        pltpu.make_async_copy(kern_hbm.at[:, k], kern.at[:, k], load_sem.at[k]) for k in range(RIM)
    ]
    loads.append(pltpu.make_async_copy(steps_hbm, steps, load_sem.at[RIM]))
    loads.append(pltpu.make_async_copy(curv_hbm, changes, load_sem.at[RIM + 1]))
    for load in loads:
        load.start()

    matrix = unscaled_gauss(rad_len, 3.0)
    high, low = halves(matrix / jnp.sum(matrix, axis=1, keepdims=True))
    rad_mat[...] = jnp.concatenate([high, high, low], axis=1)
    matrix = unscaled_gauss(lat_len, 4.0)
    high, low = halves(matrix / jnp.sum(matrix, axis=0, keepdims=True))
    lat_mat[...] = jnp.concatenate([high, high, low], axis=0)
    gram_tile[...] = jnp.zeros_like(gram_tile)
    late_tile[...] = jnp.zeros_like(late_tile)
    table[...] = jnp.zeros_like(table)

    core = e + 1 - 2 * lax.rem(e, 2)
    far = lax.rem(e + 2, n_e)
    core_far = lax.rem(core + 2, n_e)

    def rows(chunk):
        return pl.ds(pl.multiple_of(chunk * part, part), part)

    def send(src, dst, send_sem, recv_sem, where):
        return pltpu.make_async_remote_copy(
            src_ref=src, dst_ref=dst, send_sem=send_sem, recv_sem=recv_sem,
            device_id=where, device_id_type=MESH,
        )

    far_copies, near_copies, x_copies, halo_copies = [], [], [], []
    for k in range(RIM):
        loads[k].wait()
        for side in range(2):
            high, low = halves(kern[side, k])
            rad[side, k] = jnp.dot(
                rad_mat[...], jnp.concatenate([high, low, high], axis=0),
                preferred_element_type=jnp.float32,
            )
        if k == 0:
            pl.semaphore_wait(barrier, n_e - 1 + n_c - 1)
        far_copies.append(send(
            rad.at[:, k, rows(core_far)], far_in.at[:, k], core_send.at[0, k], core_recv.at[0, k],
            {"event": core},
        ))
        far_copies[-1].start()
    for k in range(RIM):
        near_copies.append(send(
            rad.at[:, k, rows(core)], near_in.at[:, k], core_send.at[1, k], core_recv.at[1, k],
            {"event": core},
        ))
        near_copies[-1].start()
    for k in range(RIM):
        far_copies[k].wait_recv()
        far_out[:, k] = rad[:, k, rows(far)] + far_in[:, k]
        x_copies.append(send(
            far_out.at[:, k], x_in.at[:, k], x_send.at[k], x_recv.at[k], {"event": far}
        ))
        x_copies[-1].start()

    slots = {pair: number for number, pair in enumerate(upper(pairs))}
    count = len(slots)
    groups = [(0, 1), (2, 3), tuple(range(4, pairs))]
    all_rows = steps.shape[1]
    tiles = all_rows // SUB
    lats = lat_len // LANES
    strip = tiles // RIM

    def gram(number):
        if number == 0:
            loads[RIM].wait()
            loads[RIM + 1].wait()

        def scale(t, _):
            place = pl.ds(pl.multiple_of(t * SUB, SUB), SUB)
            for i in range(pairs):
                changes[i, place, :] = changes[i, place, :] * steps[i, place, :]
            return 0

        lax.fori_loop(number * strip, (number + 1) * strip, scale, 0, unroll=2)
        for group in groups:
            wanted = [(i, j) for i in group for j in range(i, pairs)]

            def body(t, sums):
                place = pl.ds(pl.multiple_of(t * SUB, SUB), SUB)
                sums = list(sums)
                for lane in range(lats):
                    across = pl.ds(lane * LANES, LANES)
                    change = {j: changes[j, place, across] for j in range(group[0], pairs)}
                    for n, i in enumerate(group):
                        step = steps[i, place, across]
                        for m, (a, b) in enumerate(wanted):
                            if a == i:
                                sums[2 * m] = sums[2 * m] + step * change[b]
                                sums[2 * m + 1] = sums[2 * m + 1] + change[i] * change[b]
                return tuple(sums)

            sums = lax.fori_loop(
                number * strip, (number + 1) * strip, body,
                tuple(jnp.zeros((SUB, LANES), jnp.float32) for _ in range(2 * len(wanted))),
            )
            for m, pair in enumerate(wanted):
                for kind in range(2):
                    place = slots[pair] + kind * count
                    if number == 0:
                        gram_acc[place] = sums[2 * m + kind]
                    else:
                        gram_acc[place] = gram_acc[place] + sums[2 * m + kind]

    def spread(src, slot_refs, sends, recvs, axis, me, size):
        copies = []
        for d in range(1, size):
            copies.append(send(
                src, slot_refs.at[d - 1], sends.at[d - 1], recvs.at[d - 1],
                {axis: lax.rem(me + d, size)},
            ))
            copies[-1].start()
        return copies

    def gathered(own, slot_refs, copies):
        total = own[...]
        for d, copy in enumerate(copies):
            copy.wait_recv()
            total = total + slot_refs[d]
        return total

    left = lax.rem(c + n_c - 1, n_c)
    right = lax.rem(c + 1, n_c)

    def arrive(k):
        near_copies[k].wait_recv()
        base = rad[:, k, rows(e)] + near_in[:, k]
        x_copies[k].wait_recv()
        whole = (base + x_in[:, k]).reshape(2 * part, lat_len)
        high, low = halves(whole)
        plane[:, k] = jnp.dot(
            jnp.concatenate([high, low, high], axis=1), lat_mat[...],
            preferred_element_type=jnp.float32,
        ).reshape(2, part, lat_len)
        halo_copies.append(send(
            plane.at[0, k], trail_in.at[k], halo_send.at[0, k], halo_recv.at[0, k], {"cuts": left}
        ))
        halo_copies.append(send(
            plane.at[1, k], lead_in.at[k], halo_send.at[1, k], halo_recv.at[1, k], {"cuts": right}
        ))
        halo_copies[-2].start()
        halo_copies[-1].start()

    gram(0)
    gram(1)
    arrive(0)
    gram(2)
    arrive(1)
    gram(3)
    ones = jnp.ones((LANES, LANES), jnp.float32)
    table[pl.ds(0, 2 * count), :] = jnp.sum(gram_acc[...], axis=1)
    gram_tile[...] = lax.dot_general(
        ones[:SUB], table[...], (((1,), (1,)), ((), ())), precision=HIGHEST,
        preferred_element_type=jnp.float32,
    )
    ge_copies = spread(gram_tile, gram_event, ge_send, ge_recv, "event", e, n_e)
    arrive(2)
    gram_part[...] = gathered(gram_tile, gram_event, ge_copies)
    gc_copies = spread(gram_part, gram_cuts, gc_send, gc_recv, "cuts", c, n_c)
    arrive(3)
    products = gathered(gram_part, gram_cuts, gc_copies)
    square = (LANES, LANES)
    on_diagonal = lax.broadcasted_iota(jnp.int32, square, 0) == lax.broadcasted_iota(jnp.int32, square, 1)
    splat[...] = jnp.dot(
        jnp.where(on_diagonal, jnp.broadcast_to(products[:1], square), 0.0), ones,
        precision=HIGHEST, preferred_element_type=jnp.float32,
    )

    def cross(i, j):
        place = slots[i, j]
        return splat[place : place + 1, :]

    def squared(i, j):
        place = count + slots[min(i, j), max(i, j)]
        return splat[place : place + 1, :]

    def unit(place):
        return (lax.broadcasted_iota(jnp.int32, (1, LANES), 1) == place).astype(jnp.float32)

    inverse = [1.0 / cross(i, i) for i in range(pairs)]
    scaling = cross(pairs - 1, pairs - 1) / squared(pairs - 1, pairs - 1)
    alphas = [None] * pairs
    for i in reversed(range(pairs)):
        row = unit(i)
        for j in range(pairs - 1, i, -1):
            row = row - cross(i, j) * alphas[j]
        alphas[i] = inverse[i] * row
    onto = []
    for i in range(pairs):
        row = unit(pairs + i)
        for j in range(pairs):
            row = row - squared(i, j) * alphas[j]
        row = scaling * row
        for j in range(i):
            row = row + cross(j, i) * onto[j]
        onto.append(alphas[i] - inverse[i] * row)
    for i in range(pairs):
        mix[i : i + 1, :] = -onto[i]
        mix[pairs + i : pairs + i + 1, :] = scaling * alphas[i]

    for copy in halo_copies:
        copy.wait_recv()
    weights = cycle_weights()
    lons = 2 * RIM
    sums = [jnp.zeros((SUB, LANES), jnp.float32) for _ in range(2 * pairs)]
    per_plane = part // SUB

    def finish(t, sums):
        sums = list(sums)
        place = pl.ds(pl.multiple_of(t * SUB, SUB), SUB)
        for lane in range(lats):
            across = pl.ds(lane * LANES, LANES)
            padded = (
                [lead_in[k, place, across] for k in range(RIM)]
                + [plane[side, k, place, across] for side in range(2) for k in range(RIM)]
                + [trail_in[k, place, across] for k in range(RIM)]
            )
            for a in range(lons):
                value = weights[RIM] * padded[a + RIM]
                for k in range(1, RIM + 1):
                    value = value + weights[RIM + k] * (padded[a + RIM - k] + padded[a + RIM + k])
                spot = pl.ds(pl.multiple_of(a * part + t * SUB, SUB), SUB)
                grad[spot, across] = value
                for i in range(pairs):
                    sums[i] = sums[i] + value * steps[i, spot, across]
                    sums[pairs + i] = sums[pairs + i] + value * changes[i, spot, across]
        return tuple(sums)

    sums = lax.fori_loop(0, per_plane, finish, tuple(sums))
    for i in range(2 * pairs):
        late_tile[i : i + 1, :] = jnp.sum(sums[i], axis=0, keepdims=True)
    le_copies = spread(late_tile, late_event, le_send, le_recv, "event", e, n_e)
    grad_out = pltpu.make_async_copy(grad, grad_hbm, out_sem.at[0])
    grad_out.start()
    late_part[...] = gathered(late_tile, late_event, le_copies)
    lc_copies = spread(late_part, late_cuts, lc_send, lc_recv, "cuts", c, n_c)
    products = gathered(late_part, late_cuts, lc_copies)
    table[pl.ds(0, 2 * pairs), :] = products
    table[pl.ds(2 * pairs, LANES - 2 * pairs), :] = jnp.zeros(
        (LANES - 2 * pairs, LANES), jnp.float32
    )
    mixed = jnp.dot(mix[...], table[...], precision=HIGHEST, preferred_element_type=jnp.float32)
    coef[...] = jnp.broadcast_to(jnp.sum(mixed, axis=1, keepdims=True), coef.shape)
    ratio = jnp.broadcast_to(-scaling, (SUB, LANES))
    factors = [jnp.broadcast_to(coef[i : i + 1, :], (SUB, LANES)) for i in range(2 * pairs)]

    def combine(t, _):
        place = pl.ds(pl.multiple_of(t * SUB, SUB), SUB)
        for lane in range(lats):
            across = pl.ds(lane * LANES, LANES)
            value = ratio * grad[place, across]
            for i in range(pairs):
                value = value + factors[i] * steps[i, place, across]
                value = value + factors[pairs + i] * changes[i, place, across]
            direc[place, across] = value
        return 0

    lax.fori_loop(0, tiles, combine, 0, unroll=4)
    dir_out = pltpu.make_async_copy(direc, dir_hbm, out_sem.at[1])
    dir_out.start()
    for copies in (far_copies, near_copies, x_copies, halo_copies, ge_copies, gc_copies, le_copies, lc_copies):
        for copy in copies:
            copy.wait_send()
    grad_out.wait()
    dir_out.wait()


def shards(kernels, steps, curvature):
    n_c, n_e = lax.axis_size("cuts"), lax.axis_size("event")
    _, lons, rad_len, lat_len = kernels.shape
    pairs = steps.shape[0]
    part = rad_len // n_e
    assert lons == 2 * RIM and n_e == 4
    all_rows = lons * part
    count = pairs * (pairs + 1)
    f32, bf16 = jnp.float32, jnp.bfloat16
    vmem, dma = pltpu.VMEM, pltpu.SemaphoreType.DMA
    half = (RIM, part, lat_len)
    whole = (2,) + half
    any_spec = pl.BlockSpec(memory_space=pl.ANY)
    out = jax.ShapeDtypeStruct((all_rows, lat_len), f32)
    late = (2 * pairs, LANES)
    gradient, direction = pl.pallas_call(
        functools.partial(kernel, (n_c, n_e, pairs, rad_len, lat_len)),
        out_shape=(out, out),
        in_specs=[any_spec] * 3,
        out_specs=(any_spec, any_spec),
        scratch_shapes=[
            vmem((2, RIM, rad_len, lat_len), f32),
            vmem((pairs, all_rows, lat_len), f32),
            vmem((pairs, all_rows, lat_len), f32),
            vmem((2, RIM, rad_len, lat_len), f32),
            vmem(whole, f32),
            vmem(whole, f32),
            vmem(whole, f32),
            vmem(whole, f32),
            vmem(whole, f32),
            vmem(half, f32),
            vmem(half, f32),
            vmem((all_rows, lat_len), f32),
            vmem((all_rows, lat_len), f32),
            vmem((rad_len, 3 * rad_len), bf16),
            vmem((3 * lat_len, lat_len), bf16),
            vmem((count, SUB, LANES), f32),
            vmem((SUB, LANES), f32),
            vmem((n_e - 1, SUB, LANES), f32),
            vmem((SUB, LANES), f32),
            vmem((n_c - 1, SUB, LANES), f32),
            vmem((LANES, LANES), f32),
            vmem((LANES, LANES), f32),
            vmem((2 * pairs, LANES), f32),
            vmem((2 * pairs, LANES), f32),
            vmem(late, f32),
            vmem((n_e - 1,) + late, f32),
            vmem(late, f32),
            vmem((n_c - 1,) + late, f32),
            dma((RIM + 2,)),
            dma((2,)),
            dma((2, RIM)),
            dma((2, RIM)),
            dma((RIM,)),
            dma((RIM,)),
            dma((2, RIM)),
            dma((2, RIM)),
            dma((n_e - 1,)),
            dma((n_e - 1,)),
            dma((n_c - 1,)),
            dma((n_c - 1,)),
            dma((n_e - 1,)),
            dma((n_e - 1,)),
            dma((n_c - 1,)),
            dma((n_c - 1,)),
        ],
        compiler_params=pltpu.CompilerParams(
            collective_id=0, has_side_effects=True, vmem_limit_bytes=32 * 1024 * 1024
        ),
    )(
        kernels.reshape(2, RIM, rad_len, lat_len),
        steps.reshape(pairs, all_rows, lat_len),
        curvature.reshape(pairs, all_rows, lat_len),
    )
    shape = (lons, part, lat_len)
    return gradient.reshape(shape), direction.reshape(shape)


def solution(mesh):
    placed = (
        P("event", "cuts", None, None),
        P(None, "cuts", "event", None),
        P(None, "cuts", "event", None),
    )
    return jax.shard_map(
        shards,
        mesh=mesh,
        in_specs=placed,
        out_specs=(P("cuts", "event", None), P("cuts", "event", None)),
        check_vma=False,
    )
```

time: 202 us -> 36.4 us (0.18)
  waiting for transfers between devices: 52.8 us -> 0 us
  blocking collectives: 39.4 us -> 0 us
  between operations: 35.5 us -> 0.65 us
  Pallas kernels: 0 us -> 29.7 us
  other arithmetic: 26.4 us -> 0 us
  matrix products: 18.9 us -> 0 us
  local copies, waits for them, and re-layouts: 23.1 us -> 5.81 us
  starting transfers between devices: 4.76 us -> 0 us
    psum x1 -> x0, blocking collectives: 39.4 us -> none  [shards(): lax.psum(jnp.dot(vectors, vectors.T, precision=lax.Precision.HIGHEST), ('...]
    psum x1 -> x0, waiting for transfers between devices: 33.3 us -> none  [shards(): summed = lax.psum(radial, 'event')]
    pallas_call x0 -> x1, Pallas kernels: none -> 29.7 us  [shards(): pl.pallas_call(functools.partial(kernel, (n_c, n_e, pairs, rad_len, lat_l...]
    dot_general x16 -> x0, other arithmetic: 20.4 us -> none  [the longest x8 10.6 us: shards(): jnp.dot(products[PAIRS + pair], weights_now, precision=lax.Precision.HIGH...]
    ppermute x2 -> x0, waiting for transfers between devices: 19.6 us -> none  [the longest x1 19.6 us: with_halo(): lax.ppermute(head, axis, [((i + 1) % count, i) for i in range(count)])]
    dot_general x4 -> x0, matrix products: 18.9 us -> none  [the longest x1 8.77 us: shards(): jnp.dot(vectors, vectors.T, precision=lax.Precision.HIGHEST)]
    unnamed x21 -> x8, local copies, waits for them, and re-layouts: 13 us -> 5.81 us
    concatenate x1 -> x0, local copies, waits for them, and re-layouts: 6.03 us -> none  [shards(): jnp.concatenate([steps.reshape(PAIRS, -1), changes.reshape(PAIRS, -1), gr...]
  transfers between devices with their start and end apart: 3 -> 0, of which waited for: 2 -> 0; matrix products, arithmetic and copies ran while one was open for 4% -> 0% of each run, Pallas kernels for 0% -> 0%
where the time goes in v1:
time: 36.4 us; the launch traced here: 36.2 us
  Pallas kernels  29.7 us (82%)
  local copies, waits for them, and re-layouts  5.81 us (16%)
  between operations  0.65 us (2%)
    pallas_call x1, Pallas kernels, shards(): pl.pallas_call(functools.partial(kernel, (n_c, n_e, pairs, rad_len, lat_l...  29.7 us
    unnamed x8, local copies, waits for them, and re-layouts  5.81 us

profile of v1, /device:TPU:0, one launch (start us, length us, event | category | flops | bytes accessed | tf_op | source)
XLA Modules:
  0.0 36.2 jit_solution(4558730047184669760)
XLA Ops:
  0.6 0.0 copy-start
  0.6 1.6 %copy-done = f32[8,8,32,256]{3,2,1,0:T(8,128)S(1)} copy-done((f32[8,8,32,256]{3,2,1,0:T(8,128)S(1)}, f32[8,8,32,256]{3,2,1,0:T(8,128)}, u32[]{:S(2)}) %copy-start) | copy-done | bytes 2097176
  2.2 0.0 copy-start.1
  2.2 1.6 %copy-done.1 = f32[8,8,32,256]{3,2,1,0:T(8,128)S(1)} copy-done((f32[8,8,32,256]{3,2,1,0:T(8,128)S(1)}, f32[8,8,32,256]{3,2,1,0:T(8,128)}, u32[]{:S(2)}) %copy-start.1) | copy-done | bytes 2097176
  3.8 0.0 copy-start.2
  3.8 1.2 %copy-done.2 = f32[1,8,128,256]{3,2,1,0:T(8,128)S(1)} copy-done((f32[1,8,128,256]{3,2,1,0:T(8,128)S(1)}, f32[1,8,128,256]{3,2,1,0:T(8,128)}, u32[]{:S(2)}) %copy-start.2) | copy-done | bytes 1048600
  5.0 29.7 %shard_map.50 = (f32[256,256]{1,0:T(8,128)S(1)}, f32[256,256]{1,0:T(8,128)S(1)}) custom-call(f32[2,4,128,256]{3,2,1,0:T(8,128)S(1)} %bitcast.7, f32[8,256,256]{2,1,0:T(8,128)S(1)} %bitcast.5, f32[8,256,256]{2,1,0:T(8,128)S(1)} %bitcast.6), custom_call_target="tpu_custom_call" | custom-call | tf_op jit(solution)/shard_map/pallas_call | solution.py:347
  34.8 0.7 %copy.7 = f32[8,32,256]{2,1,0:T(8,128)} copy(f32[8,32,256]{2,1,0:T(8,128)S(1)} %bitcast.9) | data formatting | bytes 524288
  35.5 0.7 %copy.8 = f32[8,32,256]{2,1,0:T(8,128)} copy(f32[8,32,256]{2,1,0:T(8,128)S(1)} %bitcast.8) | data formatting | bytes 524288
Async XLA Ops:
  0.6 1.6 %copy-start = (f32[8,8,32,256]{3,2,1,0:T(8,128)S(1)}, f32[8,8,32,256]{3,2,1,0:T(8,128)}, u32[]{:S(2)}) copy-start(f32[8,8,32,256]{3,2,1,0:T(8,128)} %param.4) | copy-start | bytes 6291460
  2.2 1.6 %copy-start.1 = (f32[8,8,32,256]{3,2,1,0:T(8,128)S(1)}, f32[8,8,32,256]{3,2,1,0:T(8,128)}, u32[]{:S(2)}) copy-start(f32[8,8,32,256]{3,2,1,0:T(8,128)} %param.5) | copy-start | bytes 6291460
  3.8 1.2 %copy-start.2 = (f32[1,8,128,256]{3,2,1,0:T(8,128)S(1)}, f32[1,8,128,256]{3,2,1,0:T(8,128)}, u32[]{:S(2)}) copy-start(f32[1,8,128,256]{3,2,1,0:T(8,128)} %param.3) | copy-start | bytes 3145732

commit v2 on v1

--- a/solution.py
+++ b/solution.py
@@ -39,22 +39,24 @@
 
 def kernel(
     sizes,
-    kern_hbm, steps_hbm, curv_hbm, grad_hbm, dir_hbm,
-    kern, steps, changes, rad, far_in, near_in, far_out, x_in, plane, lead_in, trail_in,
-    grad, direc, rad_mat, lat_mat, gram_acc, gram_tile, gram_event, gram_part, gram_cuts,
-    table, splat, mix, coef, late_tile, late_event, late_part, late_cuts,
-    load_sem, out_sem, core_send, core_recv, x_send, x_recv, halo_send, halo_recv,
-    ge_send, ge_recv, gc_send, gc_recv, le_send, le_recv, lc_send, lc_recv,
+    kern_hbm, steps_hbm, curv_hbm, grad, steps, changes, coef,
+    kern, rad, far_in, near_in, far_out, x_in, plane, lead_in, trail_in,
+    rad_mat, lat_mat, gram_acc, gram_row, gram_all,
+    table, splat, mix, late_row, late_all,
+    load_sem, core_send, core_recv, x_send, x_recv, halo_send, halo_recv,
+    gram_send, gram_recv, late_send, late_recv,
 ):
     n_c, n_e, pairs, rad_len, lat_len = sizes
     part = rad_len // n_e
     c = lax.axis_index("cuts")
     e = lax.axis_index("event")
     barrier = pltpu.get_barrier_semaphore()
-    for d in range(1, n_e):
-        pl.semaphore_signal(barrier, 1, device_id={"event": lax.rem(e + d, n_e)}, device_id_type=MESH)
-    for d in range(1, n_c):
-        pl.semaphore_signal(barrier, 1, device_id={"cuts": lax.rem(c + d, n_c)}, device_id_type=MESH)
+    others = [
+        {"cuts": lax.rem(c + d // n_e, n_c), "event": lax.rem(e + d % n_e, n_e)}
+        for d in range(1, n_c * n_e)
+    ]
+    for other in others:
+        pl.semaphore_signal(barrier, 1, device_id=other, device_id_type=MESH)
 
     loads = [
         pltpu.make_async_copy(kern_hbm.at[:, k], kern.at[:, k], load_sem.at[k]) for k in range(RIM)
@@ -70,8 +72,6 @@
     matrix = unscaled_gauss(lat_len, 4.0)
     high, low = halves(matrix / jnp.sum(matrix, axis=0, keepdims=True))
     lat_mat[...] = jnp.concatenate([high, high, low], axis=0)
-    gram_tile[...] = jnp.zeros_like(gram_tile)
-    late_tile[...] = jnp.zeros_like(late_tile)
     table[...] = jnp.zeros_like(table)
 
     core = e + 1 - 2 * lax.rem(e, 2)
@@ -97,7 +97,7 @@
                 preferred_element_type=jnp.float32,
             )
         if k == 0:
-            pl.semaphore_wait(barrier, n_e - 1 + n_c - 1)
+            pl.semaphore_wait(barrier, len(others))
         far_copies.append(send(
             rad.at[:, k, rows(core_far)], far_in.at[:, k], core_send.at[0, k], core_recv.at[0, k],
             {"event": core},
@@ -166,22 +166,17 @@
                     else:
                         gram_acc[place] = gram_acc[place] + sums[2 * m + kind]
 
-    def spread(src, slot_refs, sends, recvs, axis, me, size):
+    def spread(row, slot_refs, sends, recvs):
         copies = []
-        for d in range(1, size):
-            copies.append(send(
-                src, slot_refs.at[d - 1], sends.at[d - 1], recvs.at[d - 1],
-                {axis: lax.rem(me + d, size)},
-            ))
+        for d, other in enumerate(others):
+            copies.append(send(row, slot_refs.at[d], sends.at[d], recvs.at[d], other))
             copies[-1].start()
         return copies
 
-    def gathered(own, slot_refs, copies):
-        total = own[...]
-        for d, copy in enumerate(copies):
+    def gathered(row, slot_refs, copies):
+        for copy in copies:
             copy.wait_recv()
-            total = total + slot_refs[d]
-        return total
+        return row[...] + jnp.sum(slot_refs[...], axis=0)
 
     left = lax.rem(c + n_c - 1, n_c)
     right = lax.rem(c + 1, n_c)
@@ -205,28 +200,26 @@
         halo_copies[-2].start()
         halo_copies[-1].start()
 
-    gram(0)
-    gram(1)
-    arrive(0)
-    gram(2)
-    arrive(1)
-    gram(3)
+    for number in range(RIM):
+        gram(number)
     ones = jnp.ones((LANES, LANES), jnp.float32)
+
+    def lane_sums(value):
+        return lax.dot_general(
+            ones[:SUB], value, (((1,), (1,)), ((), ())), precision=HIGHEST,
+            preferred_element_type=jnp.float32,
+        )[:1]
+
     table[pl.ds(0, 2 * count), :] = jnp.sum(gram_acc[...], axis=1)
-    gram_tile[...] = lax.dot_general(
-        ones[:SUB], table[...], (((1,), (1,)), ((), ())), precision=HIGHEST,
-        preferred_element_type=jnp.float32,
-    )
-    ge_copies = spread(gram_tile, gram_event, ge_send, ge_recv, "event", e, n_e)
-    arrive(2)
-    gram_part[...] = gathered(gram_tile, gram_event, ge_copies)
-    gc_copies = spread(gram_part, gram_cuts, gc_send, gc_recv, "cuts", c, n_c)
-    arrive(3)
-    products = gathered(gram_part, gram_cuts, gc_copies)
+    gram_row[...] = lane_sums(table[...])
+    gram_copies = spread(gram_row, gram_all, gram_send, gram_recv)
+    for k in range(RIM):
+        arrive(k)
+    products = gathered(gram_row, gram_all, gram_copies)
     square = (LANES, LANES)
     on_diagonal = lax.broadcasted_iota(jnp.int32, square, 0) == lax.broadcasted_iota(jnp.int32, square, 1)
     splat[...] = jnp.dot(
-        jnp.where(on_diagonal, jnp.broadcast_to(products[:1], square), 0.0), ones,
+        jnp.where(on_diagonal, jnp.broadcast_to(products, square), 0.0), ones,
         precision=HIGHEST, preferred_element_type=jnp.float32,
     )
 
@@ -239,7 +232,7 @@
         return splat[place : place + 1, :]
 
     def unit(place):
-        return (lax.broadcasted_iota(jnp.int32, (1, LANES), 1) == place).astype(jnp.float32)
+        return (lax.broadcasted_iota(jnp.int32, (1, LANES), 1) // SUB == place).astype(jnp.float32)
 
     inverse = [1.0 / cross(i, i) for i in range(pairs)]
     scaling = cross(pairs - 1, pairs - 1) / squared(pairs - 1, pairs - 1)
@@ -292,25 +285,29 @@
 
     sums = lax.fori_loop(0, per_plane, finish, tuple(sums))
     for i in range(2 * pairs):
-        late_tile[i : i + 1, :] = jnp.sum(sums[i], axis=0, keepdims=True)
-    le_copies = spread(late_tile, late_event, le_send, le_recv, "event", e, n_e)
-    grad_out = pltpu.make_async_copy(grad, grad_hbm, out_sem.at[0])
+        table[i * SUB : (i + 1) * SUB, :] = sums[i]
+    late_row[...] = lane_sums(table[...])
+    late_copies = spread(late_row, late_all, late_send, late_recv)
+    products = gathered(late_row, late_all, late_copies)
+    mixed = jnp.sum(mix[...] * products, axis=1, keepdims=True)
+    coef[pl.ds(0, 2 * pairs), :] = jnp.broadcast_to(mixed, (2 * pairs, LANES))
+    coef[pl.ds(2 * pairs, SUB), :] = jnp.broadcast_to(-scaling, (SUB, LANES))
+    for copies in (far_copies, near_copies, x_copies, halo_copies, gram_copies, late_copies):
+        for copy in copies:
+            copy.wait_send()
+
+
+def combine_kernel(pairs, blocks, grad, steps, changes, coef, grad_hbm, dir_hbm, direc, sems):
+    grad_out = pltpu.make_async_copy(grad, grad_hbm, sems.at[blocks])
     grad_out.start()
-    late_part[...] = gathered(late_tile, late_event, le_copies)
-    lc_copies = spread(late_part, late_cuts, lc_send, lc_recv, "cuts", c, n_c)
-    products = gathered(late_part, late_cuts, lc_copies)
-    table[pl.ds(0, 2 * pairs), :] = products
-    table[pl.ds(2 * pairs, LANES - 2 * pairs), :] = jnp.zeros(
-        (LANES - 2 * pairs, LANES), jnp.float32
-    )
-    mixed = jnp.dot(mix[...], table[...], precision=HIGHEST, preferred_element_type=jnp.float32)
-    coef[...] = jnp.broadcast_to(jnp.sum(mixed, axis=1, keepdims=True), coef.shape)
-    ratio = jnp.broadcast_to(-scaling, (SUB, LANES))
+    all_rows, lat_len = grad.shape
+    ratio = jnp.broadcast_to(coef[2 * pairs : 2 * pairs + 1, :], (SUB, LANES))
     factors = [jnp.broadcast_to(coef[i : i + 1, :], (SUB, LANES)) for i in range(2 * pairs)]
+    tiles = all_rows // SUB // blocks
 
     def combine(t, _):
         place = pl.ds(pl.multiple_of(t * SUB, SUB), SUB)
-        for lane in range(lats):
+        for lane in range(lat_len // LANES):
             across = pl.ds(lane * LANES, LANES)
             value = ratio * grad[place, across]
             for i in range(pairs):
@@ -319,14 +316,15 @@
             direc[place, across] = value
         return 0
 
-    lax.fori_loop(0, tiles, combine, 0, unroll=4)
-    dir_out = pltpu.make_async_copy(direc, dir_hbm, out_sem.at[1])
-    dir_out.start()
-    for copies in (far_copies, near_copies, x_copies, halo_copies, ge_copies, gc_copies, le_copies, lc_copies):
-        for copy in copies:
-            copy.wait_send()
+    copies = []
+    for block in range(blocks):
+        lax.fori_loop(block * tiles, (block + 1) * tiles, combine, 0, unroll=4)
+        place = pl.ds(block * tiles * SUB, tiles * SUB)
+        copies.append(pltpu.make_async_copy(direc.at[place], dir_hbm.at[place], sems.at[block]))
+        copies[-1].start()
     grad_out.wait()
-    dir_out.wait()
+    for copy in copies:
+        copy.wait()
 
 
 def shards(kernels, steps, curvature):
@@ -341,18 +339,23 @@
     vmem, dma = pltpu.VMEM, pltpu.SemaphoreType.DMA
     half = (RIM, part, lat_len)
     whole = (2,) + half
+    vmem_spec = pl.BlockSpec(memory_space=pltpu.VMEM)
     any_spec = pl.BlockSpec(memory_space=pl.ANY)
     out = jax.ShapeDtypeStruct((all_rows, lat_len), f32)
-    late = (2 * pairs, LANES)
-    gradient, direction = pl.pallas_call(
+    others = n_c * n_e - 1
+    assert 2 * pairs * SUB == LANES
+    staged = pl.pallas_call(
         functools.partial(kernel, (n_c, n_e, pairs, rad_len, lat_len)),
-        out_shape=(out, out),
+        out_shape=(
+            vmem((all_rows, lat_len), f32),
+            vmem((pairs, all_rows, lat_len), f32),
+            vmem((pairs, all_rows, lat_len), f32),
+            vmem((2 * pairs + SUB, LANES), f32),
+        ),
         in_specs=[any_spec] * 3,
-        out_specs=(any_spec, any_spec),
+        out_specs=(vmem_spec,) * 4,
         scratch_shapes=[
             vmem((2, RIM, rad_len, lat_len), f32),
-            vmem((pairs, all_rows, lat_len), f32),
-            vmem((pairs, all_rows, lat_len), f32),
             vmem((2, RIM, rad_len, lat_len), f32),
             vmem(whole, f32),
             vmem(whole, f32),
@@ -361,48 +364,45 @@
             vmem(whole, f32),
             vmem(half, f32),
             vmem(half, f32),
-            vmem((all_rows, lat_len), f32),
-            vmem((all_rows, lat_len), f32),
             vmem((rad_len, 3 * rad_len), bf16),
             vmem((3 * lat_len, lat_len), bf16),
             vmem((count, SUB, LANES), f32),
-            vmem((SUB, LANES), f32),
-            vmem((n_e - 1, SUB, LANES), f32),
-            vmem((SUB, LANES), f32),
-            vmem((n_c - 1, SUB, LANES), f32),
+            vmem((1, LANES), f32),
+            vmem((others, 1, LANES), f32),
             vmem((LANES, LANES), f32),
             vmem((LANES, LANES), f32),
             vmem((2 * pairs, LANES), f32),
-            vmem((2 * pairs, LANES), f32),
-            vmem(late, f32),
-            vmem((n_e - 1,) + late, f32),
-            vmem(late, f32),
-            vmem((n_c - 1,) + late, f32),
+            vmem((1, LANES), f32),
+            vmem((others, 1, LANES), f32),
             dma((RIM + 2,)),
-            dma((2,)),
             dma((2, RIM)),
             dma((2, RIM)),
             dma((RIM,)),
             dma((RIM,)),
             dma((2, RIM)),
             dma((2, RIM)),
-            dma((n_e - 1,)),
-            dma((n_e - 1,)),
-            dma((n_c - 1,)),
-            dma((n_c - 1,)),
-            dma((n_e - 1,)),
-            dma((n_e - 1,)),
-            dma((n_c - 1,)),
-            dma((n_c - 1,)),
+            dma((others,)),
+            dma((others,)),
+            dma((others,)),
+            dma((others,)),
         ],
         compiler_params=pltpu.CompilerParams(
-            collective_id=0, has_side_effects=True, vmem_limit_bytes=32 * 1024 * 1024
+            collective_id=0, has_side_effects=True, vmem_limit_bytes=61905306
         ),
     )(
         kernels.reshape(2, RIM, rad_len, lat_len),
         steps.reshape(pairs, all_rows, lat_len),
         curvature.reshape(pairs, all_rows, lat_len),
     )
+    blocks = 4
+    gradient, direction = pl.pallas_call(
+        functools.partial(combine_kernel, pairs, blocks),
+        out_shape=(out, out),
+        in_specs=[vmem_spec] * 4,
+        out_specs=(any_spec, any_spec),
+        scratch_shapes=[vmem((all_rows, lat_len), f32), dma((blocks + 1,))],
+        compiler_params=pltpu.CompilerParams(vmem_limit_bytes=2 * 1024 * 1024),
+    )(*staged)
     shape = (lons, part, lat_len)
     return gradient.reshape(shape), direction.reshape(shape)
 

time: 36.4 us -> 29.2 us (0.80)
  local copies, waits for them, and re-layouts: 5.81 us -> 0 us
  Pallas kernels: 29.7 us -> 28.4 us
    unnamed x8 -> x0, local copies, waits for them, and re-layouts: 5.81 us -> none
    pallas_call x1, Pallas kernels: 29.7 us -> 27.4 us  [shards(): pl.pallas_call(functools.partial(kernel, (n_c, n_e, pairs, rad_len, lat_l...]
    pallas_call x0 -> x1, Pallas kernels: none -> 1.05 us  [shards(): pl.pallas_call(functools.partial(combine_kernel, pairs, blocks), out_shap...]
where the time goes in v2:
time: 29.2 us; the launch traced here: 29.1 us
  Pallas kernels  28.4 us (97%)
  between operations  0.64 us (2%)
    pallas_call x1, Pallas kernels, shards(): pl.pallas_call(functools.partial(kernel, (n_c, n_e, pairs, rad_len, lat_l...  27.4 us
    pallas_call x1, Pallas kernels, shards(): pl.pallas_call(functools.partial(combine_kernel, pairs, blocks), out_shap...  1.05 us

profile of v2, /device:TPU:0, one launch (start us, length us, event | category | flops | bytes accessed | tf_op | source)
XLA Modules:
  0.0 29.1 jit_solution(12149126856565048956)
XLA Ops:
  0.6 27.4 %shard_map.50 = (f32[256,256]{1,0:T(8,128)S(1)}, f32[8,256,256]{2,1,0:T(8,128)S(1)}, f32[8,256,256]{2,1,0:T(8,128)S(1)}, f32[24,128]{1,0:T(8,128)S(1)}) custom-call(f32[2,4,128,256]{3,2,1,0:T(8,128)} %bitcast.7, f32[8,256,256]{2,1,0:T(8,128)} %bitcast.5, f32[8,256,256]{2,1,0:T(8,128)} %bitcast.6), custom_call_target="tpu_custom_call" | custom-call | tf_op jit(solution)/shard_map/pallas_call | solution.py:347
  28.0 1.0 %shard_map.51 = (f32[256,256]{1,0:T(8,128)}, f32[256,256]{1,0:T(8,128)}) custom-call(f32[256,256]{1,0:T(8,128)S(1)} %get-tuple-element.8.grad, f32[8,256,256]{2,1,0:T(8,128)S(1)} %get-tuple-element.9.steps, f32[8,256,256]{2,1,0:T(8,128)S(1)} %get-tuple-element.10.changes, f32[24,128]{1,0:T(8,128)S(1)} %get-tuple-element.11.coef), custom_call_target="tpu_custom_call" | custom-call | tf_op jit(solution)/shard_map/pallas_call | solution.py:398

commit v3 on v2

--- a/solution.py
+++ b/solution.py
@@ -9,6 +9,7 @@
 from jax.sharding import PartitionSpec as P
 
 RIM = 4
+SPLIT = 2
 LANES = 128
 SUB = 8
 MESH = pl.DeviceIdType.MESH
@@ -40,7 +41,7 @@
 def kernel(
     sizes,
     kern_hbm, steps_hbm, curv_hbm, grad, steps, changes, coef,
-    kern, rad, far_in, near_in, far_out, x_in, plane, lead_in, trail_in,
+    kern, rad, far_in, near_in, far_out, x_in, plane, halo_in,
     rad_mat, lat_mat, gram_acc, gram_row, gram_all,
     table, splat, mix, late_row, late_all,
     load_sem, core_send, core_recv, x_send, x_recv, halo_send, halo_recv,
@@ -96,8 +97,8 @@
                 rad_mat[...], jnp.concatenate([high, low, high], axis=0),
                 preferred_element_type=jnp.float32,
             )
-        if k == 0:
-            pl.semaphore_wait(barrier, len(others))
+    pl.semaphore_wait(barrier, len(others))
+    for k in range(RIM):
         far_copies.append(send(
             rad.at[:, k, rows(core_far)], far_in.at[:, k], core_send.at[0, k], core_recv.at[0, k],
             {"event": core},
@@ -109,11 +110,23 @@
             {"event": core},
         ))
         near_copies[-1].start()
-    for k in range(RIM):
-        far_copies[k].wait_recv()
-        far_out[:, k] = rad[:, k, rows(far)] + far_in[:, k]
+    strips = part // SUB
+    step_k = RIM // SPLIT
+    pieces = [(h, g) for h in range(strips) for g in range(SPLIT)]
+
+    def strip_rows(chunk, h):
+        return pl.ds(pl.multiple_of(chunk * part + h * SUB, SUB), SUB)
+
+    for h, g in pieces:
+        ks = pl.ds(g * step_k, step_k)
+        if h == 0:
+            for k in range(g * step_k, (g + 1) * step_k):
+                far_copies[k].wait_recv()
+        here = pl.ds(h * SUB, SUB)
+        far_out[:, ks, here] = rad[:, ks, strip_rows(far, h)] + far_in[:, ks, here]
         x_copies.append(send(
-            far_out.at[:, k], x_in.at[:, k], x_send.at[k], x_recv.at[k], {"event": far}
+            far_out.at[:, ks, here], x_in.at[:, ks, here], x_send.at[h, g], x_recv.at[h, g],
+            {"event": far},
         ))
         x_copies[-1].start()
 
@@ -178,30 +191,64 @@
             copy.wait_recv()
         return row[...] + jnp.sum(slot_refs[...], axis=0)
 
-    left = lax.rem(c + n_c - 1, n_c)
-    right = lax.rem(c + 1, n_c)
-
-    def arrive(k):
-        near_copies[k].wait_recv()
-        base = rad[:, k, rows(e)] + near_in[:, k]
-        x_copies[k].wait_recv()
-        whole = (base + x_in[:, k]).reshape(2 * part, lat_len)
-        high, low = halves(whole)
-        plane[:, k] = jnp.dot(
-            jnp.concatenate([high, low, high], axis=1), lat_mat[...],
-            preferred_element_type=jnp.float32,
-        ).reshape(2, part, lat_len)
-        halo_copies.append(send(
-            plane.at[0, k], trail_in.at[k], halo_send.at[0, k], halo_recv.at[0, k], {"cuts": left}
-        ))
-        halo_copies.append(send(
-            plane.at[1, k], lead_in.at[k], halo_send.at[1, k], halo_recv.at[1, k], {"cuts": right}
-        ))
-        halo_copies[-2].start()
-        halo_copies[-1].start()
-
-    for number in range(RIM):
-        gram(number)
+    def arrive(h):
+        here = pl.ds(h * SUB, SUB)
+        for g in range(SPLIT):
+            ks = pl.ds(g * step_k, step_k)
+            if h == 0:
+                for k in range(g * step_k, (g + 1) * step_k):
+                    near_copies[k].wait_recv()
+            base = rad[:, ks, strip_rows(e, h)] + near_in[:, ks, here]
+            x_copies[h * SPLIT + g].wait_recv()
+            whole = (base + x_in[:, ks, here]).reshape(2 * step_k * SUB, lat_len)
+            high, low = halves(whole)
+            plane[:, ks, here] = jnp.dot(
+                jnp.concatenate([high, low, high], axis=1), lat_mat[...],
+                preferred_element_type=jnp.float32,
+            ).reshape(2, step_k, SUB, lat_len)
+            odd = lax.rem(c, 2)
+            for side in (odd, 1 - odd):
+                halo_copies.append(send(
+                    plane.at[side, ks, here], halo_in.at[side, ks, here],
+                    halo_send.at[side, h, g], halo_recv.at[side, h, g],
+                    {"cuts": lax.rem(c + n_c - 1 + 2 * side, n_c)},
+                ))
+                halo_copies[-1].start()
+
+    weights = cycle_weights()
+    lons = 2 * RIM
+
+    def finish(h):
+        for copy in halo_copies[2 * SPLIT * h : 2 * SPLIT * (h + 1)]:
+            copy.wait_recv()
+        sums = [None] * (2 * pairs)
+        for lane in range(lats):
+            place, across = pl.ds(h * SUB, SUB), pl.ds(lane * LANES, LANES)
+            padded = (
+                [halo_in[1, k, place, across] for k in range(RIM)]
+                + [plane[side, k, place, across] for side in range(2) for k in range(RIM)]
+                + [halo_in[0, k, place, across] for k in range(RIM)]
+            )
+            for a in range(lons):
+                value = weights[RIM] * padded[a + RIM]
+                for k in range(1, RIM + 1):
+                    value = value + weights[RIM + k] * (padded[a + RIM - k] + padded[a + RIM + k])
+                spot = pl.ds(a * part + h * SUB, SUB)
+                grad[spot, across] = value
+                for i in range(pairs):
+                    for n, vector in ((i, steps), (pairs + i, changes)):
+                        term = value * vector[i, spot, across]
+                        sums[n] = term if sums[n] is None else sums[n] + term
+        for n in range(2 * pairs):
+            place = pl.ds(n * SUB, SUB)
+            table[place, :] = sums[n] if h == 0 else table[place, :] + sums[n]
+
+    gram(0)
+    gram(1)
+    arrive(0)
+    gram(2)
+    arrive(1)
+    gram(3)
     ones = jnp.ones((LANES, LANES), jnp.float32)
 
     def lane_sums(value):
@@ -213,8 +260,17 @@
     table[pl.ds(0, 2 * count), :] = jnp.sum(gram_acc[...], axis=1)
     gram_row[...] = lane_sums(table[...])
     gram_copies = spread(gram_row, gram_all, gram_send, gram_recv)
-    for k in range(RIM):
-        arrive(k)
+    for h in range(2, strips):
+        arrive(h)
+    for h in range(strips):
+        finish(h)
+    first, _ = halves(table[...])
+    second, third = halves(table[...] - first.astype(jnp.float32))
+    late_row[...] = lax.dot_general(
+        jnp.ones((SUB, 3 * LANES), jnp.bfloat16), jnp.concatenate([first, second, third], axis=1),
+        (((1,), (1,)), ((), ())), preferred_element_type=jnp.float32,
+    )[:1]
+    late_copies = spread(late_row, late_all, late_send, late_recv)
     products = gathered(gram_row, gram_all, gram_copies)
     square = (LANES, LANES)
     on_diagonal = lax.broadcasted_iota(jnp.int32, square, 0) == lax.broadcasted_iota(jnp.int32, square, 1)
@@ -255,39 +311,6 @@
         mix[i : i + 1, :] = -onto[i]
         mix[pairs + i : pairs + i + 1, :] = scaling * alphas[i]
 
-    for copy in halo_copies:
-        copy.wait_recv()
-    weights = cycle_weights()
-    lons = 2 * RIM
-    sums = [jnp.zeros((SUB, LANES), jnp.float32) for _ in range(2 * pairs)]
-    per_plane = part // SUB
-
-    def finish(t, sums):
-        sums = list(sums)
-        place = pl.ds(pl.multiple_of(t * SUB, SUB), SUB)
-        for lane in range(lats):
-            across = pl.ds(lane * LANES, LANES)
-            padded = (
-                [lead_in[k, place, across] for k in range(RIM)]
-                + [plane[side, k, place, across] for side in range(2) for k in range(RIM)]
-                + [trail_in[k, place, across] for k in range(RIM)]
-            )
-            for a in range(lons):
-                value = weights[RIM] * padded[a + RIM]
-                for k in range(1, RIM + 1):
-                    value = value + weights[RIM + k] * (padded[a + RIM - k] + padded[a + RIM + k])
-                spot = pl.ds(pl.multiple_of(a * part + t * SUB, SUB), SUB)
-                grad[spot, across] = value
-                for i in range(pairs):
-                    sums[i] = sums[i] + value * steps[i, spot, across]
-                    sums[pairs + i] = sums[pairs + i] + value * changes[i, spot, across]
-        return tuple(sums)
-
-    sums = lax.fori_loop(0, per_plane, finish, tuple(sums))
-    for i in range(2 * pairs):
-        table[i * SUB : (i + 1) * SUB, :] = sums[i]
-    late_row[...] = lane_sums(table[...])
-    late_copies = spread(late_row, late_all, late_send, late_recv)
     products = gathered(late_row, late_all, late_copies)
     mixed = jnp.sum(mix[...] * products, axis=1, keepdims=True)
     coef[pl.ds(0, 2 * pairs), :] = jnp.broadcast_to(mixed, (2 * pairs, LANES))
@@ -362,8 +385,7 @@
             vmem(whole, f32),
             vmem(whole, f32),
             vmem(whole, f32),
-            vmem(half, f32),
-            vmem(half, f32),
+            vmem(whole, f32),
             vmem((rad_len, 3 * rad_len), bf16),
             vmem((3 * lat_len, lat_len), bf16),
             vmem((count, SUB, LANES), f32),
@@ -377,10 +399,10 @@
             dma((RIM + 2,)),
             dma((2, RIM)),
             dma((2, RIM)),
-            dma((RIM,)),
-            dma((RIM,)),
-            dma((2, RIM)),
-            dma((2, RIM)),
+            dma((part // SUB, SPLIT)),
+            dma((part // SUB, SPLIT)),
+            dma((2, part // SUB, SPLIT)),
+            dma((2, part // SUB, SPLIT)),
             dma((others,)),
             dma((others,)),
             dma((others,)),

time: 29.2 us -> 28.7 us (0.983)
  Pallas kernels: 28.4 us -> 27.9 us
    pallas_call x1, Pallas kernels: 27.4 us -> 26.9 us  [shards(): pl.pallas_call(functools.partial(kernel, (n_c, n_e, pairs, rad_len, lat_l...]
where the time goes in v3:
time: 28.7 us; the launch traced here: 28.6 us
  Pallas kernels  27.9 us (97%)
  between operations  0.64 us (2%)
    pallas_call x1, Pallas kernels, shards(): pl.pallas_call(functools.partial(kernel, (n_c, n_e, pairs, rad_len, lat_l...  26.9 us
    pallas_call x1, Pallas kernels, shards(): pl.pallas_call(functools.partial(combine_kernel, pairs, blocks), out_shap...  1.05 us

profile of v3, /device:TPU:0, one launch (start us, length us, event | category | flops | bytes accessed | tf_op | source)
XLA Modules:
  0.0 28.6 jit_solution(13814434262770059454)
XLA Ops:
  0.6 26.9 %shard_map.50 = (f32[256,256]{1,0:T(8,128)S(1)}, f32[8,256,256]{2,1,0:T(8,128)S(1)}, f32[8,256,256]{2,1,0:T(8,128)S(1)}, f32[24,128]{1,0:T(8,128)S(1)}) custom-call(f32[2,4,128,256]{3,2,1,0:T(8,128)} %bitcast.7, f32[8,256,256]{2,1,0:T(8,128)} %bitcast.5, f32[8,256,256]{2,1,0:T(8,128)} %bitcast.6), custom_call_target="tpu_custom_call" | custom-call | tf_op jit(solution)/shard_map/pallas_call | solution.py:370
  27.5 1.0 %shard_map.51 = (f32[256,256]{1,0:T(8,128)}, f32[256,256]{1,0:T(8,128)}) custom-call(f32[256,256]{1,0:T(8,128)S(1)} %get-tuple-element.8.grad, f32[8,256,256]{2,1,0:T(8,128)S(1)} %get-tuple-element.9.steps, f32[8,256,256]{2,1,0:T(8,128)S(1)} %get-tuple-element.10.changes, f32[24,128]{1,0:T(8,128)S(1)} %get-tuple-element.11.coef), custom_call_target="tpu_custom_call" | custom-call | tf_op jit(solution)/shard_map/pallas_call | solution.py:420
